TPU v7x, 32 devices: a whole 2x2x4 slice. The times are simulated.
32 devices in a mesh: data: 4 (over z), model: 8 (over y, x, core).
Axes of the slice: x: 2, y: 2, z: 4, core: 2. Of those that a mesh axis runs over, the one named last changes fastest.
Arguments:
- x_saved: bfloat16 [2, 4, 4096, 2048], P(None, 'data', 'model')
- h_saved: bfloat16 [2, 4, 4096, 8192], P(None, 'data', None, 'model')
- w_up: bfloat16 [2, 2048, 8192], P(None, None, 'model')
- w_down: bfloat16 [2, 8192, 2048], P(None, 'model')
- grad_out: bfloat16 [4, 4096, 2048], P('data', 'model')
Outputs:
- output 1: bfloat16 [4, 4096, 2048], P('data', 'model')
- output 2: float32 [2, 2048, 8192], P(None, None, 'model')
- output 3: float32 [2, 8192, 2048], P(None, 'model')
All inputs are finite; a program needn't handle non-finite values.
Results may differ from a plain program's by a relative error of at most 0.0134317.
Values are sent between devices in bfloat16 or wider.
A program may use at most 1 GiB of HBM per device.

v0:
```python
import jax
import jax.numpy as jnp
from jax import lax
from jax.sharding import PartitionSpec as P


def gelu_parts(pre_act):
    inner = 0.7978845608028654 * (pre_act + 0.044715 * pre_act * pre_act * pre_act)
    tanh_val = jnp.tanh(inner)
    gelu_out = 0.5 * pre_act * (1.0 + tanh_val)
    gelu_slope = 0.5 * (1.0 + tanh_val) + 0.5 * pre_act * (1.0 - tanh_val * tanh_val) * 0.7978845608028654 * (1.0 + 0.134145 * pre_act * pre_act)
    return gelu_out, gelu_slope


def solution(mesh):
    def device_step(x_saved, h_saved, w_up, w_down, grad_out):
        layers = w_up.shape[0]
        grad_next = grad_out
        up_list = []
        down_list = []
        for layer in reversed(range(layers)):
            grad_full = lax.all_gather(grad_next, "model", axis=1, tiled=True)
            d_act = jnp.einsum("bsd,fd->bsf", grad_full, w_down[layer], preferred_element_type=jnp.float32)
            gelu_out, gelu_slope = gelu_parts(h_saved[layer].astype(jnp.float32))
            d_pre = (d_act * gelu_slope).astype(jnp.bfloat16)
            part_sum = jnp.einsum("bsf,df->bsd", d_pre, w_up[layer], preferred_element_type=jnp.float32).astype(jnp.bfloat16)
            branch = lax.psum_scatter(part_sum, "model", scatter_dimension=1, tiled=True)
            new_grad = (grad_next.astype(jnp.float32) + branch.astype(jnp.float32)).astype(jnp.bfloat16)
            x_full = lax.all_gather(x_saved[layer], "model", axis=1, tiled=True)
            grad_down = jnp.einsum("bsf,bsd->fd", gelu_out.astype(jnp.bfloat16), grad_full, preferred_element_type=jnp.float32)
            grad_up = jnp.einsum("bsd,bsf->df", x_full, d_pre, preferred_element_type=jnp.float32)
            up_list.append(grad_up)
            down_list.append(grad_down)
            grad_next = new_grad
        up_total = lax.psum(jnp.stack(up_list[::-1]), "data")
        down_total = lax.psum(jnp.stack(down_list[::-1]), "data")
        return grad_next, up_total, down_total

    return jax.shard_map(
        device_step,
        mesh=mesh,
        in_specs=(P(None, "data", "model", None), P(None, "data", None, "model"), P(None, None, "model"), P(None, "model", None), P("data", "model", None)),
        out_specs=(P("data", "model", None), P(None, None, "model"), P(None, "model", None)),
        check_vma=False,
    )
```

profile of v0, /device:TPU:0, one launch (start us, length us, event | category | flops | bytes accessed | tf_op | source)
XLA Modules:
  0.0 1811.0 jit_solution(10551248732824936203)
XLA Ops:
  7.2 0.0 all-gather.7.cloned.1.call-start
  7.2 0.7 all-gather.7.cloned.1.call-update
  7.9 0.0 reduce-scatter.3.cloned.1.call-start
  7.9 94.3 %all-gather.7.cloned.1.call-done = bf16[1,4096,2048]{2,1,0:T(8,128)(2,1)} async-done(((bf16[1,512,2048]{2,1,0:T(8,128)(2,1)}), bf16[1,4096,2048]{2,1,0:T(8,128)(2,1)}) %all-gather.7.cloned.1.call-update) | async-done | bytes 16777232 | tf_op jit(solution)/shard_map/all_gather | solution.py:22
  102.3 31.9 %fusion.21 = bf16[4096,1024]{1,0:T(8,128)(2,1)S(1)} fusion(bf16[1,4096,2048]{2,1,0:T(8,128)(2,1)} %all-gather.7.cloned.1.call-done, bf16[2,1,4096,1024]{3,2,1,0:T(8,128)(2,1)} %param.6, bf16[2,1024,2048]{2,1,0:T(8,128)(2,1)} %param.8), kind=kOutput, calls=%fused_computation.33 | convolution fusion | flops 17263755264 | bytes 37748736 | tf_op jit(solution)/shard_map/bsd,fd->bsf/dot_general | solution.py:23
  134.2 0.0 copy-start.3
  134.2 3.4 copy-done.3
  137.6 22.4 %convert_bitcast_fusion.3 = bf16[1,4096,2048]{2,1,0:T(8,128)(2,1)} fusion(bf16[4096,1024]{1,0:T(8,128)(2,1)S(1)} %fusion.21, bf16[2,2048,1024]{2,1,0:T(8,128)(2,1)} %param.7), kind=kOutput, calls=%fused_computation.69 | convolution fusion | flops 17188257792 | bytes 29360128 | tf_op jit(solution)/shard_map/bsf,df->bsd/dot_general | solution.py:26
  160.0 0.0 copy-start.1
  160.0 0.0 reduce-scatter.3.cloned.1.call-update
  160.1 0.3 all-gather.9.cloned.1.call-start
  160.4 115.1 %reduce-scatter.3.cloned.1.call-done = bf16[1,512,2048]{2,1,0:T(8,128)(2,1)} async-done(((bf16[1,4096,2048]{2,1,0:T(8,128)(2,1)}), bf16[1,512,2048]{2,1,0:T(8,128)(2,1)}) %reduce-scatter.3.cloned.1.call-update) | async-done | bytes 2097168 | tf_op jit(solution)/shard_map/reduce_scatter | solution.py:27
  275.5 0.0 copy-done.1
  275.5 3.7 add_convert_fusion.1
  279.2 0.0 all-gather.9.cloned.1.call-update
  279.2 0.0 all-gather.13.cloned.1.call-start
  279.2 4.9 fusion.104
  284.1 0.0 all-gather.13.cloned.1.call-update
  284.1 0.0 all-gather.11.cloned.1.call-start
  284.2 0.5 all-gather.11.cloned.1.call-update
  284.7 0.0 reduce-scatter.5.cloned.1.call-start
  284.8 84.2 %all-gather.9.cloned.1.call-done = bf16[1,4096,2048]{2,1,0:T(8,128)(2,1)} async-done(((bf16[1,512,2048]{2,1,0:T(8,128)(2,1)}), bf16[1,4096,2048]{2,1,0:T(8,128)(2,1)}) %all-gather.9.cloned.1.call-update) | async-done | bytes 16777232 | tf_op jit(solution)/shard_map/all_gather | solution.py:22
  369.0 31.9 %fusion.35 = bf16[4096,1024]{1,0:T(8,128)(2,1)S(1)} fusion(bf16[1,4096,2048]{2,1,0:T(8,128)(2,1)} %all-gather.9.cloned.1.call-done, bf16[2,1,4096,1024]{3,2,1,0:T(8,128)(2,1)} %param.6, bf16[2,1024,2048]{2,1,0:T(8,128)(2,1)} %param.8), kind=kOutput, calls=%fused_computation.47 | convolution fusion | flops 17263755264 | bytes 37748736 | tf_op jit(solution)/shard_map/bsd,fd->bsf/dot_general | solution.py:23
  400.9 0.0 copy-start.4
  400.9 3.2 copy-done.4
  404.2 22.4 %convert_bitcast_fusion.2 = bf16[1,4096,2048]{2,1,0:T(8,128)(2,1)} fusion(bf16[4096,1024]{1,0:T(8,128)(2,1)S(1)} %fusion.35, bf16[2,2048,1024]{2,1,0:T(8,128)(2,1)} %param.7), kind=kOutput, calls=%fused_computation.68 | convolution fusion | flops 17188257792 | bytes 29360128 | tf_op jit(solution)/shard_map/bsf,df->bsd/dot_general | solution.py:26
  426.6 0.0 reduce-scatter.5.cloned.1.call-update
  426.6 9.8 all-reduce.3.cloned.1.call-start
  436.4 24.0 %all-gather.13.cloned.1.call-done = bf16[1,1,4096,2048]{3,2,1,0:T(8,128)(2,1)} async-done(((bf16[1,1,512,2048]{3,2,1,0:T(8,128)(2,1)}), bf16[1,1,4096,2048]{3,2,1,0:T(8,128)(2,1)}) %all-gather.13.cloned.1.call-update) | async-done | bytes 16777232 | tf_op jit(solution)/shard_map/all_gather | solution.py:29
  460.4 24.2 %fusion.85 = f32[1,2048,1024]{1,2,0:T(8,128)} fusion(bf16[4096,1024]{1,0:T(8,128)(2,1)} %copy-done.3, bf16[1,1,4096,2048]{3,2,1,0:T(8,128)(2,1)} %all-gather.13.cloned.1.call-done), kind=kOutput, calls=%fused_computation.85 | convolution fusion | flops 17179869184 | bytes 33554432 | tf_op jit(solution)/shard_map/bsd,bsf->df/dot_general | solution.py:31
  484.6 31.4 %fusion.72 = f32[1,1024,2048]{2,1,0:T(8,128)} fusion(bf16[1,4096,2048]{2,1,0:T(8,128)(2,1)} %all-gather.7.cloned.1.call-done, bf16[2,1,4096,1024]{3,2,1,0:T(8,128)(2,1)} %param.6), kind=kOutput, calls=%fused_computation.82 | convolution fusion | flops 17221812224 | bytes 33554432 | tf_op jit(solution)/shard_map/bsf,bsd->fd/dot_general | solution.py:30
  515.9 35.9 %all-gather.11.cloned.1.call-done = bf16[1,1,4096,2048]{3,2,1,0:T(8,128)(2,1)} async-done(((bf16[1,1,512,2048]{3,2,1,0:T(8,128)(2,1)}), bf16[1,1,4096,2048]{3,2,1,0:T(8,128)(2,1)}) %all-gather.11.cloned.1.call-update) | async-done | bytes 16777232 | tf_op jit(solution)/shard_map/all_gather | solution.py:29
  551.8 0.0 copy-start.2
  551.8 22.9 %fusion.82 = f32[1,2048,1024]{1,2,0:T(8,128)S(1)} fusion(bf16[4096,1024]{1,0:T(8,128)(2,1)} %copy-done.4, bf16[1,1,4096,2048]{3,2,1,0:T(8,128)(2,1)} %all-gather.11.cloned.1.call-done), kind=kOutput, calls=%fused_computation.84 | convolution fusion | flops 17179869184 | bytes 33554432 | tf_op jit(solution)/shard_map/bsd,bsf->df/dot_general | solution.py:31
  574.7 0.0 copy-done.2
  574.7 0.0 slice-start
  574.7 6.6 pad_maximum_fusion
  581.3 0.0 slice-start.1
  581.3 31.6 %fusion.77 = f32[1,1024,2048]{2,1,0:T(8,128)} fusion(bf16[1,4096,2048]{2,1,0:T(8,128)(2,1)} %all-gather.9.cloned.1.call-done, bf16[2,1,4096,1024]{3,2,1,0:T(8,128)(2,1)} %param.6), kind=kOutput, calls=%fused_computation.83 | convolution fusion | flops 17221812224 | bytes 33554432 | tf_op jit(solution)/shard_map/bsf,bsd->fd/dot_general | solution.py:30
  612.9 0.0 slice-done
  612.9 0.0 slice-done.1
  612.9 9.9 pad_maximum_fusion.1
  622.8 0.0 copy-start
  622.8 0.0 all-reduce.3.cloned.1.call-update
  622.9 48.2 %reduce-scatter.5.cloned.1.call-done = bf16[1,512,2048]{2,1,0:T(8,128)(2,1)} async-done(((bf16[1,4096,2048]{2,1,0:T(8,128)(2,1)}), bf16[1,512,2048]{2,1,0:T(8,128)(2,1)}) %reduce-scatter.5.cloned.1.call-update) | async-done | bytes 2097168 | tf_op jit(solution)/shard_map/reduce_scatter | solution.py:27
  671.1 0.0 copy-done
  671.1 3.7 add_convert_fusion
  674.8 1099.2 %all-reduce.3.cloned.1.call-done = (f32[2,2048,1024]{1,2,0:T(8,128)}, f32[2,1024,2048]{2,1,0:T(8,128)}) async-done(((f32[2,2048,1024]{1,2,0:T(8,128)}, f32[2,1024,2048]{2,1,0:T(8,128)}), (f32[2,2048,1024]{1,2,0:T(8,128)}, f32[2,1024,2048]{2,1,0:T(8,128)})) %all-reduce.3.cloned.1.call-update) | async-done | bytes 33554448 | tf_op jit(solution)/shard_map/psum | solution.py:35
  1774.0 18.0 copy.8
  1792.0 11.8 copy.11
  (1 shorter events, 0.0 us)
Async XLA Ops:
  7.2 95.1 %all-gather.7.cloned.1.call-start = ((), (), s32[]{:S(2)}) async-start(), calls=%async_computation.2 | async-start | bytes 18874368 | tf_op jit(solution)/shard_map/all_gather | solution.py:22
  7.9 267.6 %reduce-scatter.3.cloned.1.call-start = ((), (), s32[]{:S(2)}) async-start(), calls=%async_computation.3 | async-start | bytes 18874368 | tf_op jit(solution)/shard_map/reduce_scatter | solution.py:27
  134.2 3.4 copy-start.3
  160.0 115.4 %copy-start.1 = (bf16[1,512,2048]{2,1,0:T(8,128)(2,1)S(1)}, bf16[1,512,2048]{2,1,0:T(8,128)(2,1)}, u32[]{:S(2)}) copy-start(bf16[1,512,2048]{2,1,0:T(8,128)(2,1)} %param.9) | copy-start | bytes 6291460
  160.1 208.9 %all-gather.9.cloned.1.call-start = ((), (), s32[]{:S(2)}) async-start(), calls=%async_computation.4 | async-start | bytes 18874368 | tf_op jit(solution)/shard_map/all_gather | solution.py:22
  279.2 181.2 %all-gather.13.cloned.1.call-start = ((), (), s32[]{:S(2)}) async-start(), calls=%async_computation.7 | async-start | bytes 18874368 | tf_op jit(solution)/shard_map/all_gather | solution.py:29
  284.1 267.7 %all-gather.11.cloned.1.call-start = ((), (), s32[]{:S(2)}) async-start(), calls=%async_computation.6 | async-start | bytes 18874368 | tf_op jit(solution)/shard_map/all_gather | solution.py:29
  284.7 386.4 %reduce-scatter.5.cloned.1.call-start = ((), (), s32[]{:S(2)}) async-start(), calls=%async_computation.5 | async-start | bytes 18874368 | tf_op jit(solution)/shard_map/reduce_scatter | solution.py:27
  400.9 3.2 copy-start.4
  426.6 1347.4 %all-reduce.3.cloned.1.call-start = ((), (), s32[]{:S(2)}) async-start(), calls=%async_computation.8 | async-start | bytes 67108864 | tf_op jit(solution)/shard_map/psum | solution.py:35
  551.8 22.9 %copy-start.2 = (f32[1,2048,1024]{1,2,0:T(8,128)S(1)}, f32[1,2048,1024]{1,2,0:T(8,128)}, u32[]{:S(2)}) copy-start(f32[1,2048,1024]{1,2,0:T(8,128)} %fusion.85) | copy-start | bytes 25165828
  574.7 38.2 %slice-start = ((s8[8388608]{0:T(1024)(128)(4,1)}), s8[4194304]{0:T(1024)(128)(4,1)S(1)}, s32[]{:S(2)}) async-start(s8[8388608]{0:T(1024)(128)(4,1)} %bitcast.162), calls=%async_computation.9 | async-start | bytes 8388608
  581.3 31.6 %slice-start.1 = ((s8[8388608]{0:T(1024)(128)(4,1)}), s8[4194304]{0:T(1024)(128)(4,1)S(1)}, s32[]{:S(2)}) async-start(s8[8388608]{0:T(1024)(128)(4,1)} %bitcast.162), calls=%async_computation.10 | async-start | bytes 8388608
  622.8 48.2 %copy-start = (bf16[1,512,2048]{2,1,0:T(8,128)(2,1)S(1)}, bf16[1,512,2048]{2,1,0:T(8,128)(2,1)}, u32[]{:S(2)}) copy-start(bf16[1,512,2048]{2,1,0:T(8,128)(2,1)} %add_convert_fusion.1) | copy-start | bytes 6291460
Sparse Core Ops, SparseCore 0:
  9.9 92.3 all-gather.6
  160.2 115.2 reduce-scatter.2
  279.3 89.6 all-gather.8
  370.7 89.6 all-gather.12
  462.1 89.6 all-gather.10
  555.8 115.2 reduce-scatter.4
  674.3 1099.6 all-reduce.2
where the time goes:
time: 1820 us; the launch traced here: 1810 us
  waiting for transfers between devices  1500 us (82%)
  matrix products  219 us (12%)
  local copies, waits for them, and re-layouts  41.3 us (2%)
  other arithmetic  23.9 us (1%)
    psum x1, waiting for transfers between devices, device_step(): up_total = lax.psum(jnp.stack(up_list[::-1]), 'data')  1100 us
    all_gather x2, waiting for transfers between devices, device_step(): grad_full = lax.all_gather(grad_next, 'model', axis=1, tiled=True)  179 us
    reduce_scatter x2, waiting for transfers between devices, device_step(): lax.psum_scatter(part_sum, 'model', scatter_dimension=1, tiled=True)  163 us
    dot_general x2, matrix products, device_step(): jnp.einsum('bsd,fd->bsf', grad_full, w_down[layer], preferred_element_typ...  63.9 us
    dot_general x2, matrix products, device_step(): jnp.einsum('bsf,bsd->fd', gelu_out.astype(jnp.bfloat16), grad_full, prefe...  63 us
    all_gather x2, waiting for transfers between devices, device_step(): x_full = lax.all_gather(x_saved[layer], 'model', axis=1, tiled=True)  59.9 us
    dot_general x2, matrix products, device_step(): jnp.einsum('bsd,bsf->df', x_full, d_pre, preferred_element_type=jnp.float32)  47 us
    dot_general x2, matrix products, device_step(): jnp.einsum('bsf,df->bsd', d_pre, w_up[layer], preferred_element_type=jnp....  44.8 us
  transfers between devices with their start and end apart: 7, of which 7 were waited for; matrix products, arithmetic and copies ran while one was open for 10% of the time, Pallas kernels for 0%

commit v1 on v0

v1 whole, which is shorter than its diff:
```python
import functools

import jax
import jax.numpy as jnp
from jax import lax
from jax.experimental import pallas as pl
from jax.experimental.pallas import tpu as pltpu
from jax.sharding import PartitionSpec as P

MESH = pl.DeviceIdType.MESH
F32, BF16 = jnp.float32, jnp.bfloat16
NT = (((1,), (1,)), ((), ()))

LAYERS = 2
CHUNKS = 8
PER_LAYER = 4 * CHUNKS
PIECES = LAYERS * PER_LAYER
SLOTS = 8
FIRST_SLOTS = 4
LAST_SLOTS = 16
LAG_SUM = 3
LAG_FREE = 5
LAG_LAST = 10
UNIT_STEP = 8
FINAL_STEP = 23


def gelu_tanh(pre):
    return jnp.tanh(0.7978845608028654 * (pre + 0.044715 * pre * pre * pre))


def gelu(pre):
    return 0.5 * pre * (1.0 + gelu_tanh(pre))


def gelu_slope(pre):
    tanh_val = gelu_tanh(pre)
    return 0.5 * (1.0 + tanh_val) + 0.5 * pre * (1.0 - tanh_val * tanh_val) * 0.7978845608028654 * (1.0 + 0.134145 * pre * pre)


def kernel(x_ref, h_ref, wu_ref, wd_ref, g_ref, gx_ref, up_ref, down_ref, gb_ref, rxh_ref,
           lt, wd, wu, cbuf, gr, hr, dh, ha, gown, xown, pm, pp, pb, rxo, rxv, zp, z1, z2,
           zs, z_r1, z_r2, z_ts, z_tl, z_rt, c1, c2, c3,
           ag_r, ag_p, ag_s, ag_f, ag_l, pp_s, pb_r, pm_s, rx_r, pbc,
           ld_c, ld_g, ld_h, ld_a, ld_w, ld_o, ld_rx, st_gx):
    rows, hidden = gown.shape
    ffn = lt.shape[1]
    half_rows = rows // 2
    cw = hidden // CHUNKS
    fb = ffn // 4
    half_ffn = ffn // 2

    me = lax.axis_index("model")
    spot = lax.axis_index("data")
    core = lax.rem(me, 2)
    px = lax.rem(me // 2, 2)
    py = me // 4
    partner = me + 1 - 2 * core
    step_x, step_y = 2 * (1 - 2 * px), 4 * (1 - 2 * py)
    peers = (me + step_x, me + step_y, me + step_x + step_y)
    is_end = jnp.logical_or(spot == 0, spot == 3)
    is_mid = jnp.logical_not(is_end)
    line_mid = jnp.where(spot < 2, 1, 2)
    line_end = jnp.where(spot < 2, 0, 3)
    line_across = 3 - spot

    def model(i):
        return {"model": i}

    def data(i):
        return {"data": i}

    def signal(sem, where):
        pl.semaphore_signal(sem, inc=1, device_id=where, device_id_type=MESH)

    def remote(src, dst, send, recv, where):
        return pltpu.make_async_remote_copy(src_ref=src, dst_ref=dst, send_sem=send, recv_sem=recv, device_id=where, device_id_type=MESH)

    def take(ref, sem):
        pltpu.make_async_copy(ref, ref, sem).wait()

    def chunk_columns(c):
        return pl.ds(pl.multiple_of(c * cw, cw), cw)

    def row_block(i):
        return pl.ds(pl.multiple_of(i * rows, rows), rows)

    def gather_keep(gid, own):
        for c in range(CHUNKS):
            pltpu.make_async_copy(own.at[:, pl.ds(c * cw, cw)], gb_ref.at[gid, c, row_block(me)], ag_l.at[gid]).start()

    def gather_send(gid, c, own):
        src = own.at[:, chunk_columns(c)]
        dst = gb_ref.at[gid, c, row_block(me)]
        for peer in peers:
            remote(src, dst, ag_s.at[gid], ag_r.at[gid, c], model(peer)).start()
        remote(src, dst, ag_s.at[gid], ag_p.at[gid, c], model(partner)).start()

    def gather_forward(gid, c):
        take(gb_ref.at[gid, c, pl.ds(0, 3 * rows)], ag_r.at[gid, c])
        for peer in peers:
            block = gb_ref.at[gid, c, row_block(peer)]
            remote(block, block, ag_f.at[gid], ag_p.at[gid, c], model(partner)).start()

    def gather_wait(gid, c):
        take(gb_ref.at[gid, c, pl.ds(0, 4 * rows)], ag_p.at[gid, c])

    def chunk_load(gid, c, slot):
        return pltpu.make_async_copy(gb_ref.at[gid, c], cbuf.at[slot], ld_c.at[slot])

    def act_load(layer, b):
        return pltpu.make_async_copy(h_ref.at[layer, row_block(b)], ha, ld_a)

    def act_block(b):
        @pl.loop(0, 4)
        def _(f):
            cols = pl.ds(pl.multiple_of(f * fb, fb), fb)
            a = gelu(ha[:, cols].astype(F32)).astype(BF16).astype(F32)
            lt[0, cols, row_block(b)] = a.T.astype(BF16)

    def weight_loads(layer):
        return (pltpu.make_async_copy(wd_ref.at[layer], wd, ld_w.at[0]), pltpu.make_async_copy(wu_ref.at[layer], wu, ld_w.at[1]))

    def unit_place(u):
        r = lax.rem(u // 2 + 1, 4)
        chip = lax.rem(py + r // 2, 2) * 2 + lax.rem(px + lax.rem(r, 2), 2)
        return r, chip

    def unit_rows(u):
        _, chip = unit_place(u)
        start = (chip * 2 + core) * rows + lax.rem(u, 2) * half_rows
        other = (chip * 2 + 1 - core) * rows + lax.rem(u, 2) * half_rows
        return tuple(pl.ds(pl.multiple_of(s, half_rows), half_rows) for s in (start, other))

    def unit_load(gid, layer, u):
        for n, block in enumerate(unit_rows(u)):
            here = pl.ds(n * half_rows, half_rows)
            for c in range(CHUNKS):
                pltpu.make_async_copy(gb_ref.at[gid, c, block], gr.at[here, pl.ds(c * cw, cw)], ld_g).start()
            pltpu.make_async_copy(h_ref.at[layer, block], hr.at[here], ld_h).start()

    def unit(lp, u):
        order = lp * 8 + u
        slot = lax.rem(order, 2)
        take(gr, ld_g)
        take(hr, ld_h)
        mine, other = unit_rows(u)

        @pl.loop(0, 4)
        def _(f):
            cols = pl.ds(pl.multiple_of(f * fb, fb), fb)
            d_act = lax.dot_general(gr[...], wd[cols, :], NT, preferred_element_type=F32)
            d_pre = (d_act * gelu_slope(hr[:, cols].astype(F32))).astype(BF16)
            dh[:, cols] = d_pre
            flipped = d_pre.astype(F32).T.astype(BF16)
            lt[1, cols, mine] = flipped[:, :half_rows]
            lt[1, cols, other] = flipped[:, half_rows:]

        @pl.when(order >= 2)
        def _():
            take(pp.at[slot], pp_s.at[slot])

            @pl.when(lax.rem(order - 2, 8) < 6)
            def _():
                take(pm.at[slot], pm_s.at[slot])

        @pl.loop(0, CHUNKS)
        def _(d):
            cols = chunk_columns(d)
            part = lax.dot_general(dh[...], wu[cols, :], NT, preferred_element_type=F32).astype(BF16)
            pm[slot, :, cols] = part[:half_rows]
            pp[slot, :, cols] = part[half_rows:]

        @pl.when(order >= 2)
        def _():
            pl.semaphore_wait(pbc, 1)

        remote(pp.at[slot], pb.at[slot], pp_s.at[slot], pb_r.at[slot], model(partner)).start()

    def unit_finish(lp, u):
        order = lp * 8 + u
        slot = lax.rem(order, 2)
        r, chip = unit_place(u)
        here = pl.ds(pl.multiple_of(lax.rem(u, 2) * half_rows, half_rows), half_rows)
        take(pb.at[slot], pb_r.at[slot])

        @pl.when(r != 0)
        def _():
            @pl.loop(0, CHUNKS)
            def _(d):
                cols = chunk_columns(d)
                pm[slot, :, cols] = (pm[slot, :, cols].astype(F32) + pb[slot, :, cols].astype(F32)).astype(BF16)

            remote(pm.at[slot], rxh_ref.at[lp, r - 1, here], pm_s.at[slot], rx_r.at[lp * 6 + (r - 1) * 2 + lax.rem(u, 2)],
                   model(chip * 2 + core)).start()

        @pl.when(r == 0)
        def _():
            @pl.loop(0, CHUNKS)
            def _(d):
                cols = chunk_columns(d)
                rxo[here, cols] = (pm[slot, :, cols].astype(F32) + pb[slot, :, cols].astype(F32)).astype(BF16)

        @pl.when(order < 8 * LAYERS - 2)
        def _():
            signal(pbc, model(partner))

    def new_gradient(lp):
        take(gb_ref.at[2 * lp, pl.ds(0, 4)], ag_s.at[2 * lp])
        for n in range(2):
            here = pl.ds(n * half_rows, half_rows)
            for r in range(3):
                take(rxv.at[r], rx_r.at[lp * 6 + r * 2 + n])
                pltpu.make_async_copy(rxh_ref.at[lp, r, here], rxv.at[r], ld_rx.at[r]).start()
            for r in range(3):
                take(rxv.at[r], ld_rx.at[r])

            @pl.loop(0, CHUNKS)
            def _(d):
                cols = chunk_columns(d)
                total = rxo[here, cols].astype(F32)
                for r in range(3):
                    total += rxv[r, :, cols].astype(F32)
                gown[here, cols] = (gown[here, cols].astype(F32) + total).astype(BF16)

    def piece_place(i):
        return LAYERS - 1 - i // PER_LAYER, lax.rem(i // (2 * CHUNKS), 2), lax.rem(i, 2 * CHUNKS) // 2, lax.rem(i, 2)

    def piece(i):
        _, phase, c, half = piece_place(i)
        slot = lax.rem(i, SLOTS)
        held = lax.rem(i // 2, 2)

        @pl.when(jnp.logical_and(is_end, i >= SLOTS))
        def _():
            take(zp.at[slot], zs.at[slot])

        part = jnp.dot(lt[phase, pl.ds(pl.multiple_of(half * half_ffn, half_ffn), half_ffn), :], cbuf[held], preferred_element_type=F32)

        @pl.when(phase == 0)
        def _():
            zp[slot] = part

        @pl.when(phase == 1)
        def _():
            zp[slot, :fb, :] = part[:fb].T
            zp[slot, fb:, :] = part[fb:].T

    def finished_copies(j):
        layer, _, c, half = piece_place(j)
        slot = lax.rem(j, SLOTS)
        f0 = half * half_ffn
        down = [(z2.at[slot], down_ref.at[layer, pl.ds(pl.multiple_of(f0, half_ffn), half_ffn), chunk_columns(c)])]
        up = [(z2.at[slot, pl.ds(b * fb, fb)], up_ref.at[layer, chunk_columns(c), pl.ds(pl.multiple_of(f0 + b * fb, fb), fb)]) for b in range(2)]
        return down, up

    def line_step(i):
        @pl.when(is_end)
        def _():
            @pl.when(i < PIECES)
            def _():
                slot, there = lax.rem(i, SLOTS), lax.rem(i, FIRST_SLOTS)

                @pl.when(i >= FIRST_SLOTS)
                def _():
                    pl.semaphore_wait(c1, 1)

                remote(zp.at[slot], z1.at[there], zs.at[slot], z_r1.at[there], data(line_mid)).start()

            j = i - LAG_LAST

            @pl.when(jnp.logical_and(j >= 0, j < PIECES))
            def _():
                take(zp.at[0], z_rt.at[lax.rem(j, LAST_SLOTS)])

                @pl.when(j + LAST_SLOTS < PIECES)
                def _():
                    signal(c3, data(line_mid))

        @pl.when(is_mid)
        def _():
            slot, there = lax.rem(i, SLOTS), lax.rem(i, FIRST_SLOTS)
            j = i - LAG_SUM
            old = lax.rem(j + SLOTS, SLOTS)

            @pl.when(i < PIECES)
            def _():
                take(z1.at[there], z_r1.at[there])
                zp[slot] = zp[slot] + z1[there]

            @pl.when(jnp.logical_and(j >= 0, j < PIECES))
            def _():
                take(z2.at[old], z_r2.at[old])
                z2[old] = z2[old] + zp[old]

            @pl.when(i < PIECES)
            def _():
                @pl.when(i + FIRST_SLOTS < PIECES)
                def _():
                    signal(c1, data(line_end))

                @pl.when(i >= SLOTS)
                def _():
                    pl.semaphore_wait(c2, 1)

                remote(zp.at[slot], z2.at[slot], zs.at[slot], z_r2.at[slot], data(line_across)).start()

            @pl.when(jnp.logical_and(j >= 0, j < PIECES))
            def _():
                take(zp.at[old], zs.at[old])

                @pl.when(j >= LAST_SLOTS)
                def _():
                    pl.semaphore_wait(c3, 1)

                down, up = finished_copies(j)
                _, phase, _, _ = piece_place(j)
                for kind, copies in enumerate((down, up)):
                    @pl.when(phase == kind)
                    def _():
                        for src, dst in copies:
                            remote(src, dst, z_ts.at[old], z_rt.at[lax.rem(j, LAST_SLOTS)], data(line_end)).start()
                            pltpu.make_async_copy(src, dst, z_tl.at[old]).start()

            k = i - LAG_FREE

            @pl.when(jnp.logical_and(k >= 0, k < PIECES))
            def _():
                free = lax.rem(k, SLOTS)
                take(z2.at[free], z_ts.at[free])
                take(z2.at[free], z_tl.at[free])

                @pl.when(k + SLOTS < PIECES)
                def _():
                    signal(c2, data(line_across))

    load_g = pltpu.make_async_copy(g_ref, gown, ld_o)
    load_g.start()
    act_load(LAYERS - 1, 0).start()
    for load in weight_loads(LAYERS - 1):
        load.start()

    barrier = pltpu.get_barrier_semaphore()
    for peer in peers + (partner,):
        signal(barrier, model(peer))

    @pl.when(is_end)
    def _():
        signal(barrier, data(line_mid))
        pl.semaphore_wait(barrier, 5)

    @pl.when(is_mid)
    def _():
        signal(barrier, data(line_end))
        signal(barrier, data(line_across))
        pl.semaphore_wait(barrier, 6)

    load_g.wait()
    for c in range(CHUNKS):
        gather_send(0, c, gown)
    gather_keep(0, gown)

    @pl.loop(0, 8)
    def _(b):
        act_load(LAYERS - 1, 0).wait()
        act_block(b)

        @pl.when(b < 7)
        def _():
            act_load(LAYERS - 1, b + 1).start()

    load_x = pltpu.make_async_copy(x_ref.at[LAYERS - 1], xown, ld_o)
    load_x.start()
    load_x.wait()
    gather_forward(0, 0)
    take(gown, ag_l.at[0])
    gather_wait(0, 0)
    chunk_load(0, 0, 0).start()

    @pl.loop(0, PIECES + LAG_LAST)
    def _(i):
        lp = i // PER_LAYER
        layer = LAYERS - 1 - lp
        il = lax.rem(i, PER_LAYER)
        odd = lax.rem(i, 2) == 1
        ggid, xgid = 2 * lp, 2 * lp + 1
        live = i < PIECES

        @pl.when(live)
        def _():
            @pl.when(jnp.logical_not(odd))
            def _():
                take(cbuf.at[0], ld_c.at[lax.rem(i // 2, 2)])

            piece(i)

        line_step(i)

        def when(cond):
            return pl.when(jnp.logical_and(live, cond))

        @when(jnp.logical_and(lp == 0, jnp.logical_and(il >= 1, il < CHUNKS)))
        def _():
            gather_forward(0, il)

        @when(il == 8)
        def _():
            gather_keep(xgid, xown)
            gather_send(xgid, 0, xown)

        @when(jnp.logical_and(odd, jnp.logical_and(il >= 9, il < 23)))
        def _():
            gather_send(xgid, (il - 7) // 2, xown)

        @when(jnp.logical_and(jnp.logical_not(odd), jnp.logical_and(il >= 14, il < 30)))
        def _():
            gather_forward(xgid, (il - 14) // 2)

        @when(jnp.logical_and(lp == 0, il == 24))
        def _():
            gather_keep(2, gown)

        @when(jnp.logical_and(lp == 0, il >= 24))
        def _():
            gather_send(2, il - 24, gown)

        @when(jnp.logical_and(i >= 27, i < 35))
        def _():
            gather_forward(2, i - 27)

        @when(jnp.logical_and(lp == 0, jnp.logical_and(il >= 1, il < CHUNKS)))
        def _():
            gather_wait(0, il)

        @when(i == 28)
        def _():
            take(gown, ag_l.at[2])

        @when(jnp.logical_and(i >= 28, i < 36))
        def _():
            gather_wait(2, i - 28)

        @when(il == 15)
        def _():
            take(xown, ag_l.at[xgid])

        @when(jnp.logical_and(odd, jnp.logical_and(il >= 15, il < 31)))
        def _():
            gather_wait(xgid, (il - 15) // 2)

        @when(jnp.logical_and(odd, i + 1 < PIECES))
        def _():
            nxt = i + 1
            chunk_load(nxt // (2 * CHUNKS), lax.rem(nxt, 2 * CHUNKS) // 2, lax.rem(nxt // 2, 2)).start()

        @when(jnp.logical_and(il > UNIT_STEP, il <= UNIT_STEP + 8))
        def _():
            unit_finish(lp, il - UNIT_STEP - 1)

        @when(il == UNIT_STEP)
        def _():
            for load in weight_loads(0):
                load.wait()

        @when(jnp.logical_and(il >= UNIT_STEP, il < UNIT_STEP + 8))
        def _():
            unit(lp, il - UNIT_STEP)

        @when(jnp.logical_and(il >= UNIT_STEP - 1, il < UNIT_STEP + 7))
        def _():
            unit_load(ggid, layer, il - UNIT_STEP + 1)

        @when(il == FINAL_STEP)
        def _():
            new_gradient(lp)

        @when(i == PER_LAYER + FINAL_STEP)
        def _():
            pltpu.make_async_copy(gown, gx_ref, st_gx).start()

        @when(jnp.logical_and(lp == 0, il == 17))
        def _():
            for load in weight_loads(0):
                load.start()

        @when(jnp.logical_and(lp == 0, il >= 16))
        def _():
            @pl.when(jnp.logical_not(odd))
            def _():
                act_load(0, (il - 16) // 2).start()

            @pl.when(odd)
            def _():
                act_load(0, 0).wait()
                act_block((il - 16) // 2)

        @when(il == 31)
        def _():
            take(gb_ref.at[xgid, pl.ds(0, 4)], ag_s.at[xgid])

            @pl.when(lp == 0)
            def _():
                load = pltpu.make_async_copy(x_ref.at[0], xown, ld_o)
                load.start()
                load.wait()

    for gid in range(2 * LAYERS):
        take(gb_ref.at[gid, pl.ds(0, 3)], ag_f.at[gid])
    for slot in range(2):
        take(pp.at[slot], pp_s.at[slot])
    take(gown, st_gx)

    @pl.when(is_end)
    def _():
        for slot in range(SLOTS):
            take(zp.at[slot], zs.at[slot])


def solution(mesh):
    def device_step(x_saved, h_saved, w_up, w_down, grad_out):
        layers, hidden, ffn = w_up.shape
        rows = grad_out.shape[1]
        tokens = h_saved.shape[2]
        cw, half_ffn = hidden // CHUNKS, ffn // 2
        half_rows = rows // 2
        any_space = pl.BlockSpec(memory_space=pl.ANY)
        dma = pltpu.SemaphoreType.DMA
        vmem = pltpu.VMEM
        grad_x, grad_up, grad_down, _, _ = pl.pallas_call(
            kernel,
            name="backward",
            out_shape=(
                jax.ShapeDtypeStruct((rows, hidden), BF16),
                jax.ShapeDtypeStruct(w_up.shape, F32),
                jax.ShapeDtypeStruct(w_down.shape, F32),
                jax.ShapeDtypeStruct((2 * layers, CHUNKS, tokens, cw), BF16),
                jax.ShapeDtypeStruct((layers, 3, rows, hidden), BF16),
            ),
            in_specs=[any_space] * 5,
            out_specs=(any_space,) * 5,
            scratch_shapes=[
                vmem((2, ffn, tokens), BF16),
                vmem((ffn, hidden), BF16),
                vmem((hidden, ffn), BF16),
                vmem((2, tokens, cw), BF16),
                vmem((rows, hidden), BF16),
                vmem((rows, ffn), BF16),
                vmem((rows, ffn), BF16),
                vmem((rows, ffn), BF16),
                vmem((rows, hidden), BF16),
                vmem((rows, hidden), BF16),
                vmem((2, half_rows, hidden), BF16),
                vmem((2, half_rows, hidden), BF16),
                vmem((2, half_rows, hidden), BF16),
                vmem((rows, hidden), BF16),
                vmem((3, half_rows, hidden), BF16),
                vmem((SLOTS, half_ffn, cw), F32),
                vmem((FIRST_SLOTS, half_ffn, cw), F32),
                vmem((SLOTS, half_ffn, cw), F32),
                dma((SLOTS,)), dma((FIRST_SLOTS,)), dma((SLOTS,)), dma((SLOTS,)), dma((SLOTS,)), dma((LAST_SLOTS,)),
                pltpu.SemaphoreType.REGULAR, pltpu.SemaphoreType.REGULAR, pltpu.SemaphoreType.REGULAR,
                dma((2 * layers, CHUNKS)), dma((2 * layers, CHUNKS)), dma((2 * layers,)), dma((2 * layers,)), dma((2 * layers,)),
                dma((2,)), dma((2,)), dma((2,)), dma((6 * layers,)), pltpu.SemaphoreType.REGULAR,
                dma((2,)), dma(()), dma(()), dma(()), dma((2,)), dma(()), dma((3,)), dma(()),
            ],
            compiler_params=pltpu.CompilerParams(collective_id=0, has_side_effects=True, vmem_limit_bytes=67043328),
        )(x_saved[:, 0], h_saved[:, 0], w_up, w_down, grad_out[0])
        return grad_x[None], grad_up, grad_down

    return jax.shard_map(
        device_step,
        mesh=mesh,
        in_specs=(P(None, "data", "model", None), P(None, "data", None, "model"), P(None, None, "model"), P(None, "model", None), P("data", "model", None)),
        out_specs=(P("data", "model", None), P(None, None, "model"), P(None, "model", None)),
        check_vma=False,
    )
```

time: 1820 us -> 977 us (0.54)
  waiting for transfers between devices: 1500 us -> 0 us
  Pallas kernels: 0 us -> 951 us
  matrix products: 219 us -> 0 us
  other arithmetic: 23.9 us -> 0.01 us
    psum x1 -> x0, waiting for transfers between devices: 1100 us -> none  [device_step(): up_total = lax.psum(jnp.stack(up_list[::-1]), 'data')]
    pallas_call x0 -> x1, Pallas kernels: none -> 951 us  [device_step(): pl.pallas_call(kernel, name='backward', out_shape=(jax.ShapeDtypeStruct((...]
    all_gather x4 -> x0, waiting for transfers between devices: 238 us -> none  [the longest x2 179 us: device_step(): grad_full = lax.all_gather(grad_next, 'model', axis=1, tiled=True)]
    dot_general x8 -> x0, matrix products: 219 us -> none  [the longest x2 63.9 us: device_step(): jnp.einsum('bsd,fd->bsf', grad_full, w_down[layer], preferred_element_typ...]
    reduce_scatter x2 -> x0, waiting for transfers between devices: 163 us -> none  [device_step(): lax.psum_scatter(part_sum, 'model', scatter_dimension=1, tiled=True)]
    unnamed x16 -> x11, local copies, waits for them, and re-layouts: 36.4 us -> 24.8 us
  transfers between devices with their start and end apart: 7 -> 0, of which waited for: 7 -> 0; matrix products, arithmetic and copies ran while one was open for 10% -> 0% of each run, Pallas kernels for 0% -> 0%
where the time goes in v1:
time: 977 us; the launch traced here: 976 us
  Pallas kernels  951 us (97%)
  local copies, waits for them, and re-layouts  24.8 us (3%)
    pallas_call x1, Pallas kernels, device_step(): pl.pallas_call(kernel, name='backward', out_shape=(jax.ShapeDtypeStruct((...  951 us
    unnamed x11, local copies, waits for them, and re-layouts  24.8 us

profile of v1, /device:TPU:0, one launch (start us, length us, event | category | flops | bytes accessed | tf_op | source)
XLA Modules:
  0.0 976.1 jit_solution(3881817612347014898)
XLA Ops:
  0.6 950.6 %backward.1 = (bf16[512,2048]{1,0:T(8,128)(2,1)}, f32[2,2048,1024]{2,1,0:T(8,128)}, f32[2,1024,2048]{2,1,0:T(8,128)}, bf16[4,8,4096,256]{3,2,1,0:T(8,128)(2,1)}, bf16[2,3,512,2048]{3,2,1,0:T(8,128)(2,1)}) custom-call(bf16[2,512,2048]{2,1,0:T(8,128)(2,1)} %bitcast.7, bf16[2,4096,1024]{2,1,0:T(8,128)(2,1)} %bitcast.4, bf16[2,2048,1024]{2,1,0:T(8,128)(2,1)} %wu_ref.1, ...), custom_call_target="tpu_custom_call" | custom-call | tf_op jit(solution)/shard_map/backward/pallas_call | solution.py:529
  951.3 0.0 slice-start
  951.3 3.3 copy.11
  954.6 0.0 slice-start.1
  954.6 0.0 slice-start.2
  954.6 0.0 slice-start.3
  954.6 13.7 %copy.12 = f32[2,2048,1024]{2,1,0:T(8,128)} copy(f32[2,2048,1024]{2,1,0:T(8,128)} %get-tuple-element.13) | data formatting | bytes 33554432
  968.3 0.0 slice-done
  968.3 0.0 slice-done.1
  968.3 0.0 slice-done.2
  968.3 1.6 slice-done.3
  969.9 6.2 copy.13
  (1 shorter events, 0.0 us)
Async XLA Ops:
  951.3 17.1 %slice-start = ((s8[16777216]{0:T(1024)(128)(4,1)}), s8[4194304]{0:T(1024)(128)(4,1)S(1)}, s32[]{:S(2)}) async-start(s8[16777216]{0:T(1024)(128)(4,1)} %bitcast.5), calls=%async_computation | async-start | bytes 8388608
  954.6 13.7 %slice-start.1 = ((s8[16777216]{0:T(1024)(128)(4,1)}), s8[4194304]{0:T(1024)(128)(4,1)S(1)}, s32[]{:S(2)}) async-start(s8[16777216]{0:T(1024)(128)(4,1)} %bitcast.5), calls=%async_computation.1 | async-start | bytes 8388608
  954.6 13.7 %slice-start.2 = ((s8[16777216]{0:T(1024)(128)(4,1)}), s8[4194304]{0:T(1024)(128)(4,1)S(1)}, s32[]{:S(2)}) async-start(s8[16777216]{0:T(1024)(128)(4,1)} %bitcast.5), calls=%async_computation.2 | async-start | bytes 8388608
  954.6 15.3 %slice-start.3 = ((s8[16777216]{0:T(1024)(128)(4,1)}), s8[4194304]{0:T(1024)(128)(4,1)S(1)}, s32[]{:S(2)}) async-start(s8[16777216]{0:T(1024)(128)(4,1)} %bitcast.5), calls=%async_computation.3 | async-start | bytes 8388608

commit v2 on v1

--- a/solution.py
+++ b/solution.py
@@ -23,6 +23,7 @@
 LAG_LAST = 10
 UNIT_STEP = 8
 FINAL_STEP = 23
+SUMS = 6
 
 
 def gelu_tanh(pre):
@@ -39,7 +40,7 @@
 
 
 def kernel(x_ref, h_ref, wu_ref, wd_ref, g_ref, gx_ref, up_ref, down_ref, gb_ref, rxh_ref,
-           lt, wd, wu, cbuf, gr, hr, dh, ha, gown, xown, pm, pp, pb, rxo, rxv, zp, z1, z2,
+           lt, wd, wu, cbuf, gr, hr, dh, ha, gown, xown, pm, pp, pb, rxo, zp, z1, z2,
            zs, z_r1, z_r2, z_ts, z_tl, z_rt, c1, c2, c3,
            ag_r, ag_p, ag_s, ag_f, ag_l, pp_s, pb_r, pm_s, rx_r, pbc,
            ld_c, ld_g, ld_h, ld_a, ld_w, ld_o, ld_rx, st_gx):
@@ -156,19 +157,21 @@
             lt[1, cols, mine] = flipped[:, :half_rows]
             lt[1, cols, other] = flipped[:, half_rows:]
 
+        kept = lax.rem(u, SUMS)
+
         @pl.when(order >= 2)
         def _():
             take(pp.at[slot], pp_s.at[slot])
 
-            @pl.when(lax.rem(order - 2, 8) < 6)
-            def _():
-                take(pm.at[slot], pm_s.at[slot])
+        @pl.when(jnp.logical_or(u >= SUMS, jnp.logical_and(lp > 0, u >= 8 - SUMS)))
+        def _():
+            take(pm.at[kept], pm_s.at[kept])
 
         @pl.loop(0, CHUNKS)
         def _(d):
             cols = chunk_columns(d)
             part = lax.dot_general(dh[...], wu[cols, :], NT, preferred_element_type=F32).astype(BF16)
-            pm[slot, :, cols] = part[:half_rows]
+            pm[kept, :, cols] = part[:half_rows]
             pp[slot, :, cols] = part[half_rows:]
 
         @pl.when(order >= 2)
@@ -180,6 +183,7 @@
     def unit_finish(lp, u):
         order = lp * 8 + u
         slot = lax.rem(order, 2)
+        kept = lax.rem(u, SUMS)
         r, chip = unit_place(u)
         here = pl.ds(pl.multiple_of(lax.rem(u, 2) * half_rows, half_rows), half_rows)
         take(pb.at[slot], pb_r.at[slot])
@@ -189,9 +193,9 @@
             @pl.loop(0, CHUNKS)
             def _(d):
                 cols = chunk_columns(d)
-                pm[slot, :, cols] = (pm[slot, :, cols].astype(F32) + pb[slot, :, cols].astype(F32)).astype(BF16)
-
-            remote(pm.at[slot], rxh_ref.at[lp, r - 1, here], pm_s.at[slot], rx_r.at[lp * 6 + (r - 1) * 2 + lax.rem(u, 2)],
+                pm[kept, :, cols] = (pm[kept, :, cols].astype(F32) + pb[slot, :, cols].astype(F32)).astype(BF16)
+
+            remote(pm.at[kept], rxh_ref.at[lp, r - 1, here], pm_s.at[kept], rx_r.at[lp * 6 + (r - 1) * 2 + lax.rem(u, 2)],
                    model(chip * 2 + core)).start()
 
         @pl.when(r == 0)
@@ -199,7 +203,7 @@
             @pl.loop(0, CHUNKS)
             def _(d):
                 cols = chunk_columns(d)
-                rxo[here, cols] = (pm[slot, :, cols].astype(F32) + pb[slot, :, cols].astype(F32)).astype(BF16)
+                rxo[here, cols] = (pm[kept, :, cols].astype(F32) + pb[slot, :, cols].astype(F32)).astype(BF16)
 
         @pl.when(order < 8 * LAYERS - 2)
         def _():
@@ -207,20 +211,22 @@
 
     def new_gradient(lp):
         take(gb_ref.at[2 * lp, pl.ds(0, 4)], ag_s.at[2 * lp])
-        for n in range(2):
-            here = pl.ds(n * half_rows, half_rows)
+        part = rows // 4
+        for n in range(4):
+            here = pl.ds(n * part, part)
             for r in range(3):
-                take(rxv.at[r], rx_r.at[lp * 6 + r * 2 + n])
-                pltpu.make_async_copy(rxh_ref.at[lp, r, here], rxv.at[r], ld_rx.at[r]).start()
+                if n % 2 == 0:
+                    take(pm.at[0], rx_r.at[lp * 6 + r * 2 + n // 2])
+                pltpu.make_async_copy(rxh_ref.at[lp, r, here], gr.at[pl.ds(r * part, part)], ld_rx.at[r]).start()
             for r in range(3):
-                take(rxv.at[r], ld_rx.at[r])
+                take(gr.at[pl.ds(0, part)], ld_rx.at[r])
 
             @pl.loop(0, CHUNKS)
             def _(d):
                 cols = chunk_columns(d)
                 total = rxo[here, cols].astype(F32)
                 for r in range(3):
-                    total += rxv[r, :, cols].astype(F32)
+                    total += gr[pl.ds(r * part, part), cols].astype(F32)
                 gown[here, cols] = (gown[here, cols].astype(F32) + total).astype(BF16)
 
     def piece_place(i):
@@ -508,6 +514,8 @@
         take(gb_ref.at[gid, pl.ds(0, 3)], ag_f.at[gid])
     for slot in range(2):
         take(pp.at[slot], pp_s.at[slot])
+    for kept in range(8 - SUMS, SUMS):
+        take(pm.at[kept], pm_s.at[kept])
     take(gown, st_gx)
 
     @pl.when(is_end)
@@ -549,18 +557,17 @@
                 vmem((rows, ffn), BF16),
                 vmem((rows, hidden), BF16),
                 vmem((rows, hidden), BF16),
-                vmem((2, half_rows, hidden), BF16),
+                vmem((SUMS, half_rows, hidden), BF16),
                 vmem((2, half_rows, hidden), BF16),
                 vmem((2, half_rows, hidden), BF16),
                 vmem((rows, hidden), BF16),
-                vmem((3, half_rows, hidden), BF16),
                 vmem((SLOTS, half_ffn, cw), F32),
                 vmem((FIRST_SLOTS, half_ffn, cw), F32),
                 vmem((SLOTS, half_ffn, cw), F32),
                 dma((SLOTS,)), dma((FIRST_SLOTS,)), dma((SLOTS,)), dma((SLOTS,)), dma((SLOTS,)), dma((LAST_SLOTS,)),
                 pltpu.SemaphoreType.REGULAR, pltpu.SemaphoreType.REGULAR, pltpu.SemaphoreType.REGULAR,
                 dma((2 * layers, CHUNKS)), dma((2 * layers, CHUNKS)), dma((2 * layers,)), dma((2 * layers,)), dma((2 * layers,)),
-                dma((2,)), dma((2,)), dma((2,)), dma((6 * layers,)), pltpu.SemaphoreType.REGULAR,
+                dma((2,)), dma((2,)), dma((SUMS,)), dma((6 * layers,)), pltpu.SemaphoreType.REGULAR,
                 dma((2,)), dma(()), dma(()), dma(()), dma((2,)), dma(()), dma((3,)), dma(()),
             ],
             compiler_params=pltpu.CompilerParams(collective_id=0, has_side_effects=True, vmem_limit_bytes=67043328),

time: 977 us -> 836 us (0.86)
  Pallas kernels: 951 us -> 808 us
    pallas_call x1, Pallas kernels: 951 us -> 808 us  [device_step(): pl.pallas_call(kernel, name='backward', out_shape=(jax.ShapeDtypeStruct((...]
where the time goes in v2:
time: 836 us; the launch traced here: 833 us
  Pallas kernels  808 us (97%)
  local copies, waits for them, and re-layouts  24.8 us (3%)
    pallas_call x1, Pallas kernels, device_step(): pl.pallas_call(kernel, name='backward', out_shape=(jax.ShapeDtypeStruct((...  808 us
    unnamed x11, local copies, waits for them, and re-layouts  24.8 us

profile of v2, /device:TPU:0, one launch (start us, length us, event | category | flops | bytes accessed | tf_op | source)
XLA Modules:
  0.0 833.1 jit_solution(1638677481706603722)
XLA Ops:
  0.6 807.7 %backward.1 = (bf16[512,2048]{1,0:T(8,128)(2,1)}, f32[2,2048,1024]{2,1,0:T(8,128)}, f32[2,1024,2048]{2,1,0:T(8,128)}, bf16[4,8,4096,256]{3,2,1,0:T(8,128)(2,1)}, bf16[2,3,512,2048]{3,2,1,0:T(8,128)(2,1)}) custom-call(bf16[2,512,2048]{2,1,0:T(8,128)(2,1)} %bitcast.7, bf16[2,4096,1024]{2,1,0:T(8,128)(2,1)} %bitcast.4, bf16[2,2048,1024]{2,1,0:T(8,128)(2,1)} %wu_ref.1, ...), custom_call_target="tpu_custom_call" | custom-call | tf_op jit(solution)/shard_map/backward/pallas_call | solution.py:537
  808.3 0.0 slice-start
  808.4 3.3 copy.11
  811.7 0.0 slice-start.1
  811.7 0.0 slice-start.2
  811.7 0.0 slice-start.3
  811.7 13.7 %copy.12 = f32[2,2048,1024]{2,1,0:T(8,128)} copy(f32[2,2048,1024]{2,1,0:T(8,128)} %get-tuple-element.13) | data formatting | bytes 33554432
  825.4 0.0 slice-done
  825.4 0.0 slice-done.1
  825.4 0.0 slice-done.2
  825.4 1.6 slice-done.3
  827.0 6.2 copy.13
  (1 shorter events, 0.0 us)
Async XLA Ops:
  808.3 17.1 %slice-start = ((s8[16777216]{0:T(1024)(128)(4,1)}), s8[4194304]{0:T(1024)(128)(4,1)S(1)}, s32[]{:S(2)}) async-start(s8[16777216]{0:T(1024)(128)(4,1)} %bitcast.5), calls=%async_computation | async-start | bytes 8388608
  811.7 13.7 %slice-start.1 = ((s8[16777216]{0:T(1024)(128)(4,1)}), s8[4194304]{0:T(1024)(128)(4,1)S(1)}, s32[]{:S(2)}) async-start(s8[16777216]{0:T(1024)(128)(4,1)} %bitcast.5), calls=%async_computation.1 | async-start | bytes 8388608
  811.7 13.7 %slice-start.2 = ((s8[16777216]{0:T(1024)(128)(4,1)}), s8[4194304]{0:T(1024)(128)(4,1)S(1)}, s32[]{:S(2)}) async-start(s8[16777216]{0:T(1024)(128)(4,1)} %bitcast.5), calls=%async_computation.2 | async-start | bytes 8388608
  811.7 15.3 %slice-start.3 = ((s8[16777216]{0:T(1024)(128)(4,1)}), s8[4194304]{0:T(1024)(128)(4,1)S(1)}, s32[]{:S(2)}) async-start(s8[16777216]{0:T(1024)(128)(4,1)} %bitcast.5), calls=%async_computation.3 | async-start | bytes 8388608

commit v3 on v2

--- a/solution.py
+++ b/solution.py
@@ -13,16 +13,18 @@
 
 LAYERS = 2
 CHUNKS = 8
-PER_LAYER = 4 * CHUNKS
+PARTS = 4
+PHASE = CHUNKS * PARTS
+PER_LAYER = 2 * PHASE
 PIECES = LAYERS * PER_LAYER
-SLOTS = 8
-FIRST_SLOTS = 4
-LAST_SLOTS = 16
-LAG_SUM = 3
-LAG_FREE = 5
-LAG_LAST = 10
+SLOTS = 16
+FIRST_SLOTS = 8
+LAST_SLOTS = 32
+LAG_SUM = 2
+LAG_FREE = 6
+LAG_LAST = 20
 UNIT_STEP = 8
-FINAL_STEP = 23
+FINAL_STEP = 46
 SUMS = 6
 
 
@@ -49,7 +51,6 @@
     half_rows = rows // 2
     cw = hidden // CHUNKS
     fb = ffn // 4
-    half_ffn = ffn // 2
 
     me = lax.axis_index("model")
     spot = lax.axis_index("data")
@@ -109,14 +110,14 @@
     def chunk_load(gid, c, slot):
         return pltpu.make_async_copy(gb_ref.at[gid, c], cbuf.at[slot], ld_c.at[slot])
 
-    def act_load(layer, b):
-        return pltpu.make_async_copy(h_ref.at[layer, row_block(b)], ha, ld_a)
-
-    def act_block(b):
+    def act_load(layer, b, ref, sem):
+        return pltpu.make_async_copy(h_ref.at[layer, row_block(b)], ref, sem)
+
+    def act_block(b, ref):
         @pl.loop(0, 4)
         def _(f):
             cols = pl.ds(pl.multiple_of(f * fb, fb), fb)
-            a = gelu(ha[:, cols].astype(F32)).astype(BF16).astype(F32)
+            a = gelu(ref[:, cols].astype(F32)).astype(BF16).astype(F32)
             lt[0, cols, row_block(b)] = a.T.astype(BF16)
 
     def weight_loads(layer):
@@ -140,9 +141,7 @@
                 pltpu.make_async_copy(gb_ref.at[gid, c, block], gr.at[here, pl.ds(c * cw, cw)], ld_g).start()
             pltpu.make_async_copy(h_ref.at[layer, block], hr.at[here], ld_h).start()
 
-    def unit(lp, u):
-        order = lp * 8 + u
-        slot = lax.rem(order, 2)
+    def unit_first(u):
         take(gr, ld_g)
         take(hr, ld_h)
         mine, other = unit_rows(u)
@@ -157,6 +156,9 @@
             lt[1, cols, mine] = flipped[:, :half_rows]
             lt[1, cols, other] = flipped[:, half_rows:]
 
+    def unit_second(lp, u):
+        order = lp * 8 + u
+        slot = lax.rem(order, 2)
         kept = lax.rem(u, SUMS)
 
         @pl.when(order >= 2)
@@ -209,39 +211,46 @@
         def _():
             signal(pbc, model(partner))
 
-    def new_gradient(lp):
-        take(gb_ref.at[2 * lp, pl.ds(0, 4)], ag_s.at[2 * lp])
+    def quarter(n):
         part = rows // 4
-        for n in range(4):
-            here = pl.ds(n * part, part)
+        return pl.ds(pl.multiple_of(n * part, part), part)
+
+    def new_gradient_load(lp, n):
+        @pl.when(lax.rem(n, 2) == 0)
+        def _():
             for r in range(3):
-                if n % 2 == 0:
-                    take(pm.at[0], rx_r.at[lp * 6 + r * 2 + n // 2])
-                pltpu.make_async_copy(rxh_ref.at[lp, r, here], gr.at[pl.ds(r * part, part)], ld_rx.at[r]).start()
+                take(pm.at[0], rx_r.at[lp * 6 + r * 2 + n // 2])
+
+        for r in range(3):
+            pltpu.make_async_copy(rxh_ref.at[lp, r, quarter(n)], gr.at[quarter(r)], ld_rx.at[r]).start()
+
+    def new_gradient(n):
+        for r in range(3):
+            take(gr.at[quarter(0)], ld_rx.at[r])
+
+        @pl.loop(0, CHUNKS)
+        def _(d):
+            cols = chunk_columns(d)
+            total = rxo[quarter(n), cols].astype(F32)
             for r in range(3):
-                take(gr.at[pl.ds(0, part)], ld_rx.at[r])
-
-            @pl.loop(0, CHUNKS)
-            def _(d):
-                cols = chunk_columns(d)
-                total = rxo[here, cols].astype(F32)
-                for r in range(3):
-                    total += gr[pl.ds(r * part, part), cols].astype(F32)
-                gown[here, cols] = (gown[here, cols].astype(F32) + total).astype(BF16)
+                total += gr[quarter(r), cols].astype(F32)
+            gown[quarter(n), cols] = (gown[quarter(n), cols].astype(F32) + total).astype(BF16)
 
     def piece_place(i):
-        return LAYERS - 1 - i // PER_LAYER, lax.rem(i // (2 * CHUNKS), 2), lax.rem(i, 2 * CHUNKS) // 2, lax.rem(i, 2)
+        return LAYERS - 1 - i // PER_LAYER, lax.rem(i // PHASE, 2), lax.rem(i, PHASE) // PARTS, lax.rem(i, PARTS)
+
+    def part_columns(n):
+        return pl.ds(pl.multiple_of(n * fb, fb), fb)
 
     def piece(i):
-        _, phase, c, half = piece_place(i)
+        _, phase, _, n = piece_place(i)
         slot = lax.rem(i, SLOTS)
-        held = lax.rem(i // 2, 2)
 
         @pl.when(jnp.logical_and(is_end, i >= SLOTS))
         def _():
             take(zp.at[slot], zs.at[slot])
 
-        part = jnp.dot(lt[phase, pl.ds(pl.multiple_of(half * half_ffn, half_ffn), half_ffn), :], cbuf[held], preferred_element_type=F32)
+        part = jnp.dot(lt[phase, part_columns(n), :], cbuf[lax.rem(i // PARTS, 2)], preferred_element_type=F32)
 
         @pl.when(phase == 0)
         def _():
@@ -249,16 +258,11 @@
 
         @pl.when(phase == 1)
         def _():
-            zp[slot, :fb, :] = part[:fb].T
-            zp[slot, fb:, :] = part[fb:].T
-
-    def finished_copies(j):
-        layer, _, c, half = piece_place(j)
-        slot = lax.rem(j, SLOTS)
-        f0 = half * half_ffn
-        down = [(z2.at[slot], down_ref.at[layer, pl.ds(pl.multiple_of(f0, half_ffn), half_ffn), chunk_columns(c)])]
-        up = [(z2.at[slot, pl.ds(b * fb, fb)], up_ref.at[layer, chunk_columns(c), pl.ds(pl.multiple_of(f0 + b * fb, fb), fb)]) for b in range(2)]
-        return down, up
+            zp[slot] = part.T
+
+    def total_place(j):
+        layer, _, c, n = piece_place(j)
+        return down_ref.at[layer, part_columns(n), chunk_columns(c)], up_ref.at[layer, chunk_columns(c), part_columns(n)]
 
     def line_step(i):
         @pl.when(is_end)
@@ -289,6 +293,16 @@
             j = i - LAG_SUM
             old = lax.rem(j + SLOTS, SLOTS)
 
+            @pl.when(jnp.logical_and(j >= 0, j < PIECES))
+            def _():
+                take(z2.at[old], z_r2.at[old])
+                z2[old] = z2[old] + zp[old]
+                take(zp.at[old], zs.at[old])
+
+                @pl.when(j >= LAST_SLOTS)
+                def _():
+                    pl.semaphore_wait(c3, 1)
+
             @pl.when(i < PIECES)
             def _():
                 take(z1.at[there], z_r1.at[there])
@@ -296,8 +310,12 @@
 
             @pl.when(jnp.logical_and(j >= 0, j < PIECES))
             def _():
-                take(z2.at[old], z_r2.at[old])
-                z2[old] = z2[old] + zp[old]
+                _, phase, _, _ = piece_place(j)
+                for kind, place in enumerate(total_place(j)):
+                    @pl.when(phase == kind)
+                    def _():
+                        remote(z2.at[old], place, z_ts.at[old], z_rt.at[lax.rem(j, LAST_SLOTS)], data(line_end)).start()
+                        pltpu.make_async_copy(z2.at[old], place, z_tl.at[old]).start()
 
             @pl.when(i < PIECES)
             def _():
@@ -311,23 +329,6 @@
 
                 remote(zp.at[slot], z2.at[slot], zs.at[slot], z_r2.at[slot], data(line_across)).start()
 
-            @pl.when(jnp.logical_and(j >= 0, j < PIECES))
-            def _():
-                take(zp.at[old], zs.at[old])
-
-                @pl.when(j >= LAST_SLOTS)
-                def _():
-                    pl.semaphore_wait(c3, 1)
-
-                down, up = finished_copies(j)
-                _, phase, _, _ = piece_place(j)
-                for kind, copies in enumerate((down, up)):
-                    @pl.when(phase == kind)
-                    def _():
-                        for src, dst in copies:
-                            remote(src, dst, z_ts.at[old], z_rt.at[lax.rem(j, LAST_SLOTS)], data(line_end)).start()
-                            pltpu.make_async_copy(src, dst, z_tl.at[old]).start()
-
             k = i - LAG_FREE
 
             @pl.when(jnp.logical_and(k >= 0, k < PIECES))
@@ -340,12 +341,12 @@
                 def _():
                     signal(c2, data(line_across))
 
+    top = LAYERS - 1
     load_g = pltpu.make_async_copy(g_ref, gown, ld_o)
     load_g.start()
-    act_load(LAYERS - 1, 0).start()
-    for load in weight_loads(LAYERS - 1):
-        load.start()
-
+    held = ((ha, ld_a), (hr, ld_h))
+    for n, (ref, sem) in enumerate(held):
+        act_load(top, n, ref, sem).start()
     barrier = pltpu.get_barrier_semaphore()
     for peer in peers + (partner,):
         signal(barrier, model(peer))
@@ -365,21 +366,24 @@
     for c in range(CHUNKS):
         gather_send(0, c, gown)
     gather_keep(0, gown)
-
-    @pl.loop(0, 8)
+    load_x = pltpu.make_async_copy(x_ref.at[top], xown, ld_o)
+    load_x.start()
+    for load in weight_loads(top):
+        load.start()
+
+    @pl.loop(0, 4)
     def _(b):
-        act_load(LAYERS - 1, 0).wait()
-        act_block(b)
-
-        @pl.when(b < 7)
-        def _():
-            act_load(LAYERS - 1, b + 1).start()
-
-    load_x = pltpu.make_async_copy(x_ref.at[LAYERS - 1], xown, ld_o)
-    load_x.start()
+        for n, (ref, sem) in enumerate(held):
+            act_load(top, 0, ref, sem).wait()
+            act_block(2 * b + n, ref)
+
+            @pl.when(b < 3)
+            def _():
+                act_load(top, 2 * b + n + 2, ref, sem).start()
+
     load_x.wait()
+    take(gown, ag_l.at[0])
     gather_forward(0, 0)
-    take(gown, ag_l.at[0])
     gather_wait(0, 0)
     chunk_load(0, 0, 0).start()
 
@@ -387,128 +391,145 @@
     def _(i):
         lp = i // PER_LAYER
         layer = LAYERS - 1 - lp
+        s = i // 2
+        sl = lax.rem(s, PER_LAYER // 2)
         il = lax.rem(i, PER_LAYER)
-        odd = lax.rem(i, 2) == 1
+        even = lax.rem(i, 2) == 0
+        odd = jnp.logical_not(even)
+        odd_pair = lax.rem(s, 2) == 1
         ggid, xgid = 2 * lp, 2 * lp + 1
         live = i < PIECES
 
         @pl.when(live)
         def _():
-            @pl.when(jnp.logical_not(odd))
-            def _():
-                take(cbuf.at[0], ld_c.at[lax.rem(i // 2, 2)])
+            @pl.when(lax.rem(i, PARTS) == 0)
+            def _():
+                take(cbuf.at[0], ld_c.at[lax.rem(i // PARTS, 2)])
 
             piece(i)
 
         line_step(i)
 
-        def when(cond):
-            return pl.when(jnp.logical_and(live, cond))
-
-        @when(jnp.logical_and(lp == 0, jnp.logical_and(il >= 1, il < CHUNKS)))
-        def _():
-            gather_forward(0, il)
-
-        @when(il == 8)
+        def when(*conds):
+            return pl.when(functools.reduce(jnp.logical_and, conds, live))
+
+        @when(even, s >= 1, s < CHUNKS)
+        def _():
+            gather_forward(0, s)
+
+        @when(odd, s >= 1, s < CHUNKS)
+        def _():
+            gather_wait(0, s)
+
+        @when(even, sl == 8)
         def _():
             gather_keep(xgid, xown)
             gather_send(xgid, 0, xown)
 
-        @when(jnp.logical_and(odd, jnp.logical_and(il >= 9, il < 23)))
-        def _():
-            gather_send(xgid, (il - 7) // 2, xown)
-
-        @when(jnp.logical_and(jnp.logical_not(odd), jnp.logical_and(il >= 14, il < 30)))
-        def _():
-            gather_forward(xgid, (il - 14) // 2)
-
-        @when(jnp.logical_and(lp == 0, il == 24))
+        @when(even, odd_pair, sl >= 9, sl < 23)
+        def _():
+            gather_send(xgid, (sl - 7) // 2, xown)
+
+        @when(even, jnp.logical_not(odd_pair), sl >= 14, sl < 30)
+        def _():
+            gather_forward(xgid, (sl - 14) // 2)
+
+        @when(odd, sl == 15)
+        def _():
+            take(xown, ag_l.at[xgid])
+
+        @when(odd, odd_pair, sl >= 15, sl < 31)
+        def _():
+            gather_wait(xgid, (sl - 15) // 2)
+
+        @when(even, s == 25)
         def _():
             gather_keep(2, gown)
 
-        @when(jnp.logical_and(lp == 0, il >= 24))
-        def _():
-            gather_send(2, il - 24, gown)
-
-        @when(jnp.logical_and(i >= 27, i < 35))
-        def _():
-            gather_forward(2, i - 27)
-
-        @when(jnp.logical_and(lp == 0, jnp.logical_and(il >= 1, il < CHUNKS)))
-        def _():
-            gather_wait(0, il)
-
-        @when(i == 28)
+        @when(even, s >= 25, s < 25 + CHUNKS)
+        def _():
+            gather_send(2, s - 25, gown)
+
+        @when(even, s >= 28, s < 28 + CHUNKS)
+        def _():
+            gather_forward(2, s - 28)
+
+        @when(odd, s == 29)
         def _():
             take(gown, ag_l.at[2])
 
-        @when(jnp.logical_and(i >= 28, i < 36))
-        def _():
-            gather_wait(2, i - 28)
-
-        @when(il == 15)
-        def _():
-            take(xown, ag_l.at[xgid])
-
-        @when(jnp.logical_and(odd, jnp.logical_and(il >= 15, il < 31)))
-        def _():
-            gather_wait(xgid, (il - 15) // 2)
-
-        @when(jnp.logical_and(odd, i + 1 < PIECES))
+        @when(odd, s >= 29, s < 29 + CHUNKS)
+        def _():
+            gather_wait(2, s - 29)
+
+        @when(lax.rem(i, PARTS) == PARTS - 1, i + 1 < PIECES)
         def _():
             nxt = i + 1
-            chunk_load(nxt // (2 * CHUNKS), lax.rem(nxt, 2 * CHUNKS) // 2, lax.rem(nxt // 2, 2)).start()
-
-        @when(jnp.logical_and(il > UNIT_STEP, il <= UNIT_STEP + 8))
-        def _():
-            unit_finish(lp, il - UNIT_STEP - 1)
-
-        @when(il == UNIT_STEP)
+            chunk_load(nxt // PHASE, lax.rem(nxt, PHASE) // PARTS, lax.rem(nxt // PARTS, 2)).start()
+
+        @when(even, sl == UNIT_STEP)
         def _():
             for load in weight_loads(0):
                 load.wait()
 
-        @when(jnp.logical_and(il >= UNIT_STEP, il < UNIT_STEP + 8))
-        def _():
-            unit(lp, il - UNIT_STEP)
-
-        @when(jnp.logical_and(il >= UNIT_STEP - 1, il < UNIT_STEP + 7))
-        def _():
-            unit_load(ggid, layer, il - UNIT_STEP + 1)
-
-        @when(il == FINAL_STEP)
-        def _():
-            new_gradient(lp)
-
-        @when(i == PER_LAYER + FINAL_STEP)
+        @when(even, sl >= UNIT_STEP, sl < UNIT_STEP + 8)
+        def _():
+            unit_first(sl - UNIT_STEP)
+
+        @when(even, sl > UNIT_STEP, sl <= UNIT_STEP + 8)
+        def _():
+            unit_finish(lp, sl - UNIT_STEP - 1)
+
+        @when(odd, sl >= UNIT_STEP - 1, sl < UNIT_STEP + 7)
+        def _():
+            unit_load(ggid, layer, sl - UNIT_STEP + 1)
+
+        @when(odd, sl >= UNIT_STEP, sl < UNIT_STEP + 8)
+        def _():
+            unit_second(lp, sl - UNIT_STEP)
+
+        @when(il == FINAL_STEP - 1)
+        def _():
+            take(gb_ref.at[ggid, pl.ds(0, 4)], ag_s.at[ggid])
+            new_gradient_load(lp, 0)
+
+        @when(il >= FINAL_STEP, il < FINAL_STEP + 4)
+        def _():
+            new_gradient(il - FINAL_STEP)
+
+            @pl.when(il < FINAL_STEP + 3)
+            def _():
+                new_gradient_load(lp, il - FINAL_STEP + 1)
+
+        @when(i == PER_LAYER + FINAL_STEP + 4)
         def _():
             pltpu.make_async_copy(gown, gx_ref, st_gx).start()
 
-        @when(jnp.logical_and(lp == 0, il == 17))
+        @when(lp == 0, even, sl == 17)
         def _():
             for load in weight_loads(0):
                 load.start()
 
-        @when(jnp.logical_and(lp == 0, il >= 16))
-        def _():
-            @pl.when(jnp.logical_not(odd))
-            def _():
-                act_load(0, (il - 16) // 2).start()
-
-            @pl.when(odd)
-            def _():
-                act_load(0, 0).wait()
-                act_block((il - 16) // 2)
-
-        @when(il == 31)
+        @when(lp == 0, even, jnp.logical_not(odd_pair), sl >= 16)
+        def _():
+            act_load(0, (sl - 16) // 2, ha, ld_a).start()
+
+        @when(lp == 0, odd, odd_pair, sl >= 16)
+        def _():
+            act_load(0, 0, ha, ld_a).wait()
+            act_block((sl - 16) // 2, ha)
+
+        @when(even, sl == 31)
         def _():
             take(gb_ref.at[xgid, pl.ds(0, 4)], ag_s.at[xgid])
 
             @pl.when(lp == 0)
             def _():
-                load = pltpu.make_async_copy(x_ref.at[0], xown, ld_o)
-                load.start()
-                load.wait()
+                pltpu.make_async_copy(x_ref.at[0], xown, ld_o).start()
+
+        @when(lp == 0, odd, sl == 31)
+        def _():
+            pltpu.make_async_copy(x_ref.at[0], xown, ld_o).wait()
 
     for gid in range(2 * LAYERS):
         take(gb_ref.at[gid, pl.ds(0, 3)], ag_f.at[gid])
@@ -529,7 +550,7 @@
         layers, hidden, ffn = w_up.shape
         rows = grad_out.shape[1]
         tokens = h_saved.shape[2]
-        cw, half_ffn = hidden // CHUNKS, ffn // 2
+        cw, fb = hidden // CHUNKS, ffn // PARTS
         half_rows = rows // 2
         any_space = pl.BlockSpec(memory_space=pl.ANY)
         dma = pltpu.SemaphoreType.DMA
@@ -561,9 +582,9 @@
                 vmem((2, half_rows, hidden), BF16),
                 vmem((2, half_rows, hidden), BF16),
                 vmem((rows, hidden), BF16),
-                vmem((SLOTS, half_ffn, cw), F32),
-                vmem((FIRST_SLOTS, half_ffn, cw), F32),
-                vmem((SLOTS, half_ffn, cw), F32),
+                vmem((SLOTS, fb, cw), F32),
+                vmem((FIRST_SLOTS, fb, cw), F32),
+                vmem((SLOTS, fb, cw), F32),
                 dma((SLOTS,)), dma((FIRST_SLOTS,)), dma((SLOTS,)), dma((SLOTS,)), dma((SLOTS,)), dma((LAST_SLOTS,)),
                 pltpu.SemaphoreType.REGULAR, pltpu.SemaphoreType.REGULAR, pltpu.SemaphoreType.REGULAR,
                 dma((2 * layers, CHUNKS)), dma((2 * layers, CHUNKS)), dma((2 * layers,)), dma((2 * layers,)), dma((2 * layers,)),

time: 836 us -> 824 us (0.986)
  Pallas kernels: 808 us -> 795 us
    pallas_call x1, Pallas kernels: 808 us -> 795 us  [device_step(): pl.pallas_call(kernel, name='backward', out_shape=(jax.ShapeDtypeStruct((...]
where the time goes in v3:
time: 824 us; the launch traced here: 820 us
  Pallas kernels  795 us (96%)
  local copies, waits for them, and re-layouts  24.8 us (3%)
    pallas_call x1, Pallas kernels, device_step(): pl.pallas_call(kernel, name='backward', out_shape=(jax.ShapeDtypeStruct((...  795 us
    unnamed x11, local copies, waits for them, and re-layouts  24.8 us

profile of v3, /device:TPU:0, one launch (start us, length us, event | category | flops | bytes accessed | tf_op | source)
XLA Modules:
  0.0 820.0 jit_solution(6507854331193363700)
XLA Ops:
  0.6 794.6 %backward.1 = (bf16[512,2048]{1,0:T(8,128)(2,1)}, f32[2,2048,1024]{2,1,0:T(8,128)}, f32[2,1024,2048]{2,1,0:T(8,128)}, bf16[4,8,4096,256]{3,2,1,0:T(8,128)(2,1)}, bf16[2,3,512,2048]{3,2,1,0:T(8,128)(2,1)}) custom-call(bf16[2,512,2048]{2,1,0:T(8,128)(2,1)} %bitcast.7, bf16[2,4096,1024]{2,1,0:T(8,128)(2,1)} %bitcast.4, bf16[2,2048,1024]{2,1,0:T(8,128)(2,1)} %wu_ref.1, ...), custom_call_target="tpu_custom_call" | custom-call | tf_op jit(solution)/shard_map/backward/pallas_call | solution.py:558
  795.2 0.0 slice-start
  795.2 3.3 copy.11
  798.5 0.0 slice-start.1
  798.5 0.0 slice-start.2
  798.5 0.0 slice-start.3
  798.5 13.7 %copy.12 = f32[2,2048,1024]{2,1,0:T(8,128)} copy(f32[2,2048,1024]{2,1,0:T(8,128)} %get-tuple-element.13) | data formatting | bytes 33554432
  812.2 0.0 slice-done
  812.3 0.0 slice-done.1
  812.3 0.0 slice-done.2
  812.3 1.6 slice-done.3
  813.8 6.2 copy.13
  (1 shorter events, 0.0 us)
Async XLA Ops:
  795.2 17.1 %slice-start = ((s8[16777216]{0:T(1024)(128)(4,1)}), s8[4194304]{0:T(1024)(128)(4,1)S(1)}, s32[]{:S(2)}) async-start(s8[16777216]{0:T(1024)(128)(4,1)} %bitcast.5), calls=%async_computation | async-start | bytes 8388608
  798.5 13.7 %slice-start.1 = ((s8[16777216]{0:T(1024)(128)(4,1)}), s8[4194304]{0:T(1024)(128)(4,1)S(1)}, s32[]{:S(2)}) async-start(s8[16777216]{0:T(1024)(128)(4,1)} %bitcast.5), calls=%async_computation.1 | async-start | bytes 8388608
  798.5 13.7 %slice-start.2 = ((s8[16777216]{0:T(1024)(128)(4,1)}), s8[4194304]{0:T(1024)(128)(4,1)S(1)}, s32[]{:S(2)}) async-start(s8[16777216]{0:T(1024)(128)(4,1)} %bitcast.5), calls=%async_computation.2 | async-start | bytes 8388608
  798.5 15.3 %slice-start.3 = ((s8[16777216]{0:T(1024)(128)(4,1)}), s8[4194304]{0:T(1024)(128)(4,1)S(1)}, s32[]{:S(2)}) async-start(s8[16777216]{0:T(1024)(128)(4,1)} %bitcast.5), calls=%async_computation.3 | async-start | bytes 8388608

commit v4 on v3

--- a/solution.py
+++ b/solution.py
@@ -44,7 +44,7 @@
 def kernel(x_ref, h_ref, wu_ref, wd_ref, g_ref, gx_ref, up_ref, down_ref, gb_ref, rxh_ref,
            lt, wd, wu, cbuf, gr, hr, dh, ha, gown, xown, pm, pp, pb, rxo, zp, z1, z2,
            zs, z_r1, z_r2, z_ts, z_tl, z_rt, c1, c2, c3,
-           ag_r, ag_p, ag_s, ag_f, ag_l, pp_s, pb_r, pm_s, rx_r, pbc,
+           ag_x, ag_y, ag_d, ag_p, ag_s, ag_f, ag_l, pp_s, pb_r, pm_s, rx_r, pbc,
            ld_c, ld_g, ld_h, ld_a, ld_w, ld_o, ld_rx, st_gx):
     rows, hidden = gown.shape
     ffn = lt.shape[1]
@@ -59,7 +59,7 @@
     py = me // 4
     partner = me + 1 - 2 * core
     step_x, step_y = 2 * (1 - 2 * px), 4 * (1 - 2 * py)
-    peers = (me + step_x, me + step_y, me + step_x + step_y)
+    near_x, near_y, far = me + step_x, me + step_y, me + step_x + step_y
     is_end = jnp.logical_or(spot == 0, spot == 3)
     is_mid = jnp.logical_not(is_end)
     line_mid = jnp.where(spot < 2, 1, 2)
@@ -94,13 +94,22 @@
     def gather_send(gid, c, own):
         src = own.at[:, chunk_columns(c)]
         dst = gb_ref.at[gid, c, row_block(me)]
-        for peer in peers:
-            remote(src, dst, ag_s.at[gid], ag_r.at[gid, c], model(peer)).start()
+        remote(src, dst, ag_s.at[gid], ag_x.at[gid, c], model(near_x)).start()
+        remote(src, dst, ag_s.at[gid], ag_y.at[gid, c], model(near_y)).start()
         remote(src, dst, ag_s.at[gid], ag_p.at[gid, c], model(partner)).start()
 
+    def gather_relay(gid, c):
+        take(gb_ref.at[gid, c, row_block(0)], ag_x.at[gid, c])
+        take(gb_ref.at[gid, c, row_block(0)], ag_y.at[gid, c])
+        for n, (source, target) in enumerate(((near_x, near_y), (near_y, near_x))):
+            @pl.when(core == n)
+            def _():
+                block = gb_ref.at[gid, c, row_block(source)]
+                remote(block, block, ag_s.at[gid], ag_d.at[gid, c], model(target)).start()
+
     def gather_forward(gid, c):
-        take(gb_ref.at[gid, c, pl.ds(0, 3 * rows)], ag_r.at[gid, c])
-        for peer in peers:
+        take(gb_ref.at[gid, c, row_block(0)], ag_d.at[gid, c])
+        for peer in (near_x, near_y, far):
             block = gb_ref.at[gid, c, row_block(peer)]
             remote(block, block, ag_f.at[gid], ag_p.at[gid, c], model(partner)).start()
 
@@ -348,7 +357,7 @@
     for n, (ref, sem) in enumerate(held):
         act_load(top, n, ref, sem).start()
     barrier = pltpu.get_barrier_semaphore()
-    for peer in peers + (partner,):
+    for peer in (near_x, near_y, far, partner):
         signal(barrier, model(peer))
 
     @pl.when(is_end)
@@ -363,8 +372,7 @@
         pl.semaphore_wait(barrier, 6)
 
     load_g.wait()
-    for c in range(CHUNKS):
-        gather_send(0, c, gown)
+    gather_send(0, 0, gown)
     gather_keep(0, gown)
     load_x = pltpu.make_async_copy(x_ref.at[top], xown, ld_o)
     load_x.start()
@@ -380,6 +388,11 @@
             @pl.when(b < 3)
             def _():
                 act_load(top, 2 * b + n + 2, ref, sem).start()
+
+        @pl.when(b == 2)
+        def _():
+            gather_relay(0, 0)
+            gather_send(0, 1, gown)
 
     load_x.wait()
     take(gown, ag_l.at[0])
@@ -397,6 +410,7 @@
         even = lax.rem(i, 2) == 0
         odd = jnp.logical_not(even)
         odd_pair = lax.rem(s, 2) == 1
+        even_pair = jnp.logical_not(odd_pair)
         ggid, xgid = 2 * lp, 2 * lp + 1
         live = i < PIECES
 
@@ -413,6 +427,14 @@
         def when(*conds):
             return pl.when(functools.reduce(jnp.logical_and, conds, live))
 
+        @when(even, s < CHUNKS - 1)
+        def _():
+            gather_relay(0, s + 1)
+
+        @when(even, s < CHUNKS - 2)
+        def _():
+            gather_send(0, s + 2, gown)
+
         @when(even, s >= 1, s < CHUNKS)
         def _():
             gather_forward(0, s)
@@ -424,15 +446,18 @@
         @when(even, sl == 8)
         def _():
             gather_keep(xgid, xown)
-            gather_send(xgid, 0, xown)
-
-        @when(even, odd_pair, sl >= 9, sl < 23)
-        def _():
-            gather_send(xgid, (sl - 7) // 2, xown)
-
-        @when(even, jnp.logical_not(odd_pair), sl >= 14, sl < 30)
-        def _():
-            gather_forward(xgid, (sl - 14) // 2)
+
+        @when(even, even_pair, sl >= 8, sl < 24)
+        def _():
+            gather_send(xgid, (sl - 8) // 2, xown)
+
+        @when(even, even_pair, sl >= 10, sl < 26)
+        def _():
+            gather_relay(xgid, (sl - 10) // 2)
+
+        @when(even, odd_pair, sl >= 13, sl < 29)
+        def _():
+            gather_forward(xgid, (sl - 13) // 2)
 
         @when(odd, sl == 15)
         def _():
@@ -450,17 +475,21 @@
         def _():
             gather_send(2, s - 25, gown)
 
-        @when(even, s >= 28, s < 28 + CHUNKS)
-        def _():
-            gather_forward(2, s - 28)
-
-        @when(odd, s == 29)
+        @when(even, s >= 27, s < 27 + CHUNKS)
+        def _():
+            gather_relay(2, s - 27)
+
+        @when(even, s >= 29, s < 29 + CHUNKS)
+        def _():
+            gather_forward(2, s - 29)
+
+        @when(odd, s == 30)
         def _():
             take(gown, ag_l.at[2])
 
-        @when(odd, s >= 29, s < 29 + CHUNKS)
-        def _():
-            gather_wait(2, s - 29)
+        @when(odd, s >= 30, s < 30 + CHUNKS)
+        def _():
+            gather_wait(2, s - 30)
 
         @when(lax.rem(i, PARTS) == PARTS - 1, i + 1 < PIECES)
         def _():
@@ -510,7 +539,7 @@
             for load in weight_loads(0):
                 load.start()
 
-        @when(lp == 0, even, jnp.logical_not(odd_pair), sl >= 16)
+        @when(lp == 0, even, even_pair, sl >= 16)
         def _():
             act_load(0, (sl - 16) // 2, ha, ld_a).start()
 
@@ -587,7 +616,8 @@
                 vmem((SLOTS, fb, cw), F32),
                 dma((SLOTS,)), dma((FIRST_SLOTS,)), dma((SLOTS,)), dma((SLOTS,)), dma((SLOTS,)), dma((LAST_SLOTS,)),
                 pltpu.SemaphoreType.REGULAR, pltpu.SemaphoreType.REGULAR, pltpu.SemaphoreType.REGULAR,
-                dma((2 * layers, CHUNKS)), dma((2 * layers, CHUNKS)), dma((2 * layers,)), dma((2 * layers,)), dma((2 * layers,)),
+                dma((2 * layers, CHUNKS)), dma((2 * layers, CHUNKS)), dma((2 * layers, CHUNKS)), dma((2 * layers, CHUNKS)),
+                dma((2 * layers,)), dma((2 * layers,)), dma((2 * layers,)),
                 dma((2,)), dma((2,)), dma((SUMS,)), dma((6 * layers,)), pltpu.SemaphoreType.REGULAR,
                 dma((2,)), dma(()), dma(()), dma(()), dma((2,)), dma(()), dma((3,)), dma(()),
             ],

time: 824 us -> 885 us (1.074)
  Pallas kernels: 795 us -> 859 us
    pallas_call x1, Pallas kernels: 795 us -> 859 us  [device_step(): pl.pallas_call(kernel, name='backward', out_shape=(jax.ShapeDtypeStruct((...]
where the time goes in v4:
time: 885 us; the launch traced here: 884 us
  Pallas kernels  859 us (97%)
  local copies, waits for them, and re-layouts  24.8 us (3%)
    pallas_call x1, Pallas kernels, device_step(): pl.pallas_call(kernel, name='backward', out_shape=(jax.ShapeDtypeStruct((...  859 us
    unnamed x11, local copies, waits for them, and re-layouts  24.8 us

profile of v4, /device:TPU:0, one launch (start us, length us, event | category | flops | bytes accessed | tf_op | source)
XLA Modules:
  0.0 884.3 jit_solution(9931534358058882158)
XLA Ops:
  0.6 858.9 %backward.1 = (bf16[512,2048]{1,0:T(8,128)(2,1)}, f32[2,2048,1024]{2,1,0:T(8,128)}, f32[2,1024,2048]{2,1,0:T(8,128)}, bf16[4,8,4096,256]{3,2,1,0:T(8,128)(2,1)}, bf16[2,3,512,2048]{3,2,1,0:T(8,128)(2,1)}) custom-call(bf16[2,512,2048]{2,1,0:T(8,128)(2,1)} %bitcast.7, bf16[2,4096,1024]{2,1,0:T(8,128)(2,1)} %bitcast.4, bf16[2,2048,1024]{2,1,0:T(8,128)(2,1)} %wu_ref.1, ...), custom_call_target="tpu_custom_call" | custom-call | tf_op jit(solution)/shard_map/backward/pallas_call | solution.py:587
  859.5 0.0 slice-start
  859.5 3.3 copy.11
  862.8 0.0 slice-start.1
  862.8 0.0 slice-start.2
  862.8 0.0 slice-start.3
  862.8 13.7 %copy.12 = f32[2,2048,1024]{2,1,0:T(8,128)} copy(f32[2,2048,1024]{2,1,0:T(8,128)} %get-tuple-element.13) | data formatting | bytes 33554432
  876.6 0.0 slice-done
  876.6 0.0 slice-done.1
  876.6 0.0 slice-done.2
  876.6 1.6 slice-done.3
  878.2 6.2 copy.13
  (1 shorter events, 0.0 us)
Async XLA Ops:
  859.5 17.1 %slice-start = ((s8[16777216]{0:T(1024)(128)(4,1)}), s8[4194304]{0:T(1024)(128)(4,1)S(1)}, s32[]{:S(2)}) async-start(s8[16777216]{0:T(1024)(128)(4,1)} %bitcast.5), calls=%async_computation | async-start | bytes 8388608
  862.8 13.7 %slice-start.1 = ((s8[16777216]{0:T(1024)(128)(4,1)}), s8[4194304]{0:T(1024)(128)(4,1)S(1)}, s32[]{:S(2)}) async-start(s8[16777216]{0:T(1024)(128)(4,1)} %bitcast.5), calls=%async_computation.1 | async-start | bytes 8388608
  862.8 13.7 %slice-start.2 = ((s8[16777216]{0:T(1024)(128)(4,1)}), s8[4194304]{0:T(1024)(128)(4,1)S(1)}, s32[]{:S(2)}) async-start(s8[16777216]{0:T(1024)(128)(4,1)} %bitcast.5), calls=%async_computation.2 | async-start | bytes 8388608
  862.8 15.3 %slice-start.3 = ((s8[16777216]{0:T(1024)(128)(4,1)}), s8[4194304]{0:T(1024)(128)(4,1)S(1)}, s32[]{:S(2)}) async-start(s8[16777216]{0:T(1024)(128)(4,1)} %bitcast.5), calls=%async_computation.3 | async-start | bytes 8388608

commit v5 on v4

--- a/solution.py
+++ b/solution.py
@@ -24,6 +24,7 @@
 LAG_FREE = 6
 LAG_LAST = 20
 UNIT_STEP = 8
+X_RUNS = ((0, 5, 5, 3, 7), (5, 3, 20, 3, 5))
 FINAL_STEP = 46
 SUMS = 6
 
@@ -443,21 +444,22 @@
         def _():
             gather_wait(0, s)
 
-        @when(even, sl == 8)
+        @when(even, sl == X_RUNS[0][2])
         def _():
             gather_keep(xgid, xown)
 
-        @when(even, even_pair, sl >= 8, sl < 24)
-        def _():
-            gather_send(xgid, (sl - 8) // 2, xown)
-
-        @when(even, even_pair, sl >= 10, sl < 26)
-        def _():
-            gather_relay(xgid, (sl - 10) // 2)
-
-        @when(even, odd_pair, sl >= 13, sl < 29)
-        def _():
-            gather_forward(xgid, (sl - 13) // 2)
+        for first, count, start, relay, forward in X_RUNS:
+            @when(even, sl >= start, sl < start + count)
+            def _():
+                gather_send(xgid, sl - start + first, xown)
+
+            @when(even, sl >= start + relay, sl < start + relay + count)
+            def _():
+                gather_relay(xgid, sl - start - relay + first)
+
+            @when(even, sl >= start + forward, sl < start + forward + count)
+            def _():
+                gather_forward(xgid, sl - start - forward + first)
 
         @when(odd, sl == 15)
         def _():

time: 885 us -> 793 us (0.90)
  Pallas kernels: 859 us -> 767 us
    pallas_call x1, Pallas kernels: 859 us -> 767 us  [device_step(): pl.pallas_call(kernel, name='backward', out_shape=(jax.ShapeDtypeStruct((...]
where the time goes in v5:
time: 793 us; the launch traced here: 792 us
  Pallas kernels  767 us (97%)
  local copies, waits for them, and re-layouts  24.8 us (3%)
    pallas_call x1, Pallas kernels, device_step(): pl.pallas_call(kernel, name='backward', out_shape=(jax.ShapeDtypeStruct((...  767 us
    unnamed x11, local copies, waits for them, and re-layouts  24.8 us

profile of v5, /device:TPU:0, one launch (start us, length us, event | category | flops | bytes accessed | tf_op | source)
XLA Modules:
  0.0 792.3 jit_solution(10309367281121869494)
XLA Ops:
  0.6 766.8 %backward.1 = (bf16[512,2048]{1,0:T(8,128)(2,1)}, f32[2,2048,1024]{2,1,0:T(8,128)}, f32[2,1024,2048]{2,1,0:T(8,128)}, bf16[4,8,4096,256]{3,2,1,0:T(8,128)(2,1)}, bf16[2,3,512,2048]{3,2,1,0:T(8,128)(2,1)}) custom-call(bf16[2,512,2048]{2,1,0:T(8,128)(2,1)} %bitcast.7, bf16[2,4096,1024]{2,1,0:T(8,128)(2,1)} %bitcast.4, bf16[2,2048,1024]{2,1,0:T(8,128)(2,1)} %wu_ref.1, ...), custom_call_target="tpu_custom_call" | custom-call | tf_op jit(solution)/shard_map/backward/pallas_call | solution.py:589
  767.5 0.0 slice-start
  767.5 3.3 copy.11
  770.8 0.0 slice-start.1
  770.8 0.0 slice-start.2
  770.8 0.0 slice-start.3
  770.8 13.7 %copy.12 = f32[2,2048,1024]{2,1,0:T(8,128)} copy(f32[2,2048,1024]{2,1,0:T(8,128)} %get-tuple-element.13) | data formatting | bytes 33554432
  784.5 0.0 slice-done
  784.5 0.0 slice-done.1
  784.5 0.0 slice-done.2
  784.5 1.6 slice-done.3
  786.1 6.2 copy.13
  (1 shorter events, 0.0 us)
Async XLA Ops:
  767.5 17.1 %slice-start = ((s8[16777216]{0:T(1024)(128)(4,1)}), s8[4194304]{0:T(1024)(128)(4,1)S(1)}, s32[]{:S(2)}) async-start(s8[16777216]{0:T(1024)(128)(4,1)} %bitcast.5), calls=%async_computation | async-start | bytes 8388608
  770.8 13.7 %slice-start.1 = ((s8[16777216]{0:T(1024)(128)(4,1)}), s8[4194304]{0:T(1024)(128)(4,1)S(1)}, s32[]{:S(2)}) async-start(s8[16777216]{0:T(1024)(128)(4,1)} %bitcast.5), calls=%async_computation.1 | async-start | bytes 8388608
  770.8 13.7 %slice-start.2 = ((s8[16777216]{0:T(1024)(128)(4,1)}), s8[4194304]{0:T(1024)(128)(4,1)S(1)}, s32[]{:S(2)}) async-start(s8[16777216]{0:T(1024)(128)(4,1)} %bitcast.5), calls=%async_computation.2 | async-start | bytes 8388608
  770.8 15.3 %slice-start.3 = ((s8[16777216]{0:T(1024)(128)(4,1)}), s8[4194304]{0:T(1024)(128)(4,1)S(1)}, s32[]{:S(2)}) async-start(s8[16777216]{0:T(1024)(128)(4,1)} %bitcast.5), calls=%async_computation.3 | async-start | bytes 8388608
